TPU v7x, 8 devices: a whole 2x2x1 slice. The times are simulated.
8 devices in a mesh: dp: 2 (over z, y), tp: 4 (over x, core).
Axes of the slice: x: 2, y: 2, z: 1, core: 2. Of those that a mesh axis runs over, the one named last changes fastest.
Arguments:
- tokens: int32 [2, 256], P('dp'), parts along dimension 0
- positions: int32 [2, 256], P('dp'), parts along dimension 0
- embed_table: bfloat16 [128256, 3072], P('tp')
- w_query: bfloat16 [3072, 24, 128], P(None, 'tp')
- w_key: bfloat16 [3072, 8, 128], P(None, 'tp')
- w_value: bfloat16 [3072, 8, 128], P(None, 'tp')
- w_out: bfloat16 [24, 128, 3072], P('tp')
- w_gate: bfloat16 [3072, 8192], P(None, 'tp')
- w_up: bfloat16 [3072, 8192], P(None, 'tp')
- w_down: bfloat16 [8192, 3072], P('tp')
- norm_pre_att: float32 [3072], replicated
- norm_post_att: float32 [3072], replicated
- norm_pre_ffw: float32 [3072], replicated
- norm_post_ffw: float32 [3072], replicated
Outputs:
- output: bfloat16 [2, 256, 3072], P('dp', 'tp'), parts along dimension 0
There are 2 independent parts. A program takes and returns all parts, laid end to end along the dimension named above; an argument that names none is the same for every part.
All inputs are finite; a program needn't handle non-finite values.
Results may differ from a plain program's by a relative error of at most 0.02.
Values are sent between devices in bfloat16 or wider.
A program may use at most 1 GiB of HBM per device.

v0:
```python
import jax
import jax.numpy as jnp
from jax import lax
from jax.sharding import PartitionSpec as P

WINDOW = 4096
QUERY_SCALE = 256.0 ** -0.5
SOFT_CAP = 50.0
NORM_EPS = 1e-6
ROPE_BASE = 10000.0


def rms_norm(hidden, norm_scale):
    hidden = hidden.astype(jnp.float32)
    mean_sq = jnp.mean(hidden * hidden, axis=-1, keepdims=True)
    return (hidden * lax.rsqrt(mean_sq + NORM_EPS) * (1.0 + norm_scale)).astype(jnp.bfloat16)


def rope_tables(positions, head_dim):
    half_dim = head_dim // 2
    inv_freq = ROPE_BASE ** (-2.0 * jnp.arange(half_dim, dtype=jnp.float32) / head_dim)
    angles = positions.astype(jnp.float32)[:, :, None] * inv_freq
    return jnp.cos(angles)[:, :, None, :], jnp.sin(angles)[:, :, None, :]


def apply_rope(states, cos_tab, sin_tab):
    half_dim = states.shape[-1] // 2
    lower_half = states[..., :half_dim]
    upper_half = states[..., half_dim:]
    return jnp.concatenate([lower_half * cos_tab - upper_half * sin_tab, upper_half * cos_tab + lower_half * sin_tab], axis=-1)


def local_attention(q_states, k_states, v_states, positions):
    seq_len = q_states.shape[1]
    q_block = min(128, seq_len)
    key_span = min(seq_len, WINDOW + q_block)

    def one_block(block_idx):
        q_start = block_idx * q_block
        k_start = jnp.maximum(q_start + q_block - key_span, 0)
        q_blk = lax.dynamic_slice_in_dim(q_states, q_start, q_block, axis=1)
        k_blk = lax.dynamic_slice_in_dim(k_states, k_start, key_span, axis=1)
        v_blk = lax.dynamic_slice_in_dim(v_states, k_start, key_span, axis=1)
        q_pos = lax.dynamic_slice_in_dim(positions, q_start, q_block, axis=1)
        k_pos = lax.dynamic_slice_in_dim(positions, k_start, key_span, axis=1)
        scores = jnp.einsum("bqkgd,blkd->bkgql", q_blk, k_blk, preferred_element_type=jnp.float32)
        capped = SOFT_CAP * jnp.tanh(scores / SOFT_CAP)
        offset = q_pos[:, :, None] - k_pos[:, None, :]
        keep_mask = (offset >= 0) & (offset < WINDOW)
        capped = jnp.where(keep_mask[:, None, None, :, :], capped, -1e30)
        att_probs = jax.nn.softmax(capped, axis=-1).astype(jnp.bfloat16)
        att_mix = jnp.einsum("bkgql,blkd->bqkgd", att_probs, v_blk, preferred_element_type=jnp.float32)
        return att_mix.astype(jnp.bfloat16)

    blocks = lax.map(one_block, jnp.arange(seq_len // q_block))
    return jnp.moveaxis(blocks, 0, 1).reshape(q_states.shape)


def decoder_layer(embeds, positions, w_query, w_key, w_value, w_out, w_gate, w_up, w_down, norm_pre_att, norm_post_att, norm_pre_ffw, norm_post_ffw):
    n_batch, seq_len = positions.shape
    model_dim = embeds.shape[-1]
    kv_local, head_dim = w_key.shape[1], w_key.shape[2]
    n_group = w_query.shape[1] // kv_local
    attn_in = lax.all_gather(rms_norm(embeds, norm_pre_att), "tp", axis=1, tiled=True)
    cos_tab, sin_tab = rope_tables(positions, head_dim)
    q_proj = jnp.einsum("bsd,dnh->bsnh", attn_in, w_query, preferred_element_type=jnp.float32)
    q_states = (apply_rope(q_proj, cos_tab, sin_tab) * QUERY_SCALE).astype(jnp.bfloat16)
    q_states = q_states.reshape(n_batch, seq_len, kv_local, n_group, head_dim)
    k_proj = jnp.einsum("bsd,dnh->bsnh", attn_in, w_key, preferred_element_type=jnp.float32)
    k_states = apply_rope(k_proj, cos_tab, sin_tab).astype(jnp.bfloat16)
    v_states = jnp.einsum("bsd,dnh->bsnh", attn_in, w_value, preferred_element_type=jnp.float32).astype(jnp.bfloat16)
    att_mix = local_attention(q_states, k_states, v_states, positions)
    w_out_grp = w_out.reshape(kv_local, n_group, head_dim, model_dim)
    att_part = jnp.einsum("bskgh,kghd->bsd", att_mix, w_out_grp, preferred_element_type=jnp.float32).astype(jnp.bfloat16)
    att_proj = lax.psum_scatter(att_part, "tp", scatter_dimension=1, tiled=True)
    resid_one = (embeds.astype(jnp.float32) + rms_norm(att_proj, norm_post_att).astype(jnp.float32)).astype(jnp.bfloat16)
    mlp_in = lax.all_gather(rms_norm(resid_one, norm_pre_ffw), "tp", axis=1, tiled=True)
    gate_pre = jnp.einsum("bsd,df->bsf", mlp_in, w_gate, preferred_element_type=jnp.float32)
    up_proj = jnp.einsum("bsd,df->bsf", mlp_in, w_up, preferred_element_type=jnp.float32)
    ffn_act = (jax.nn.gelu(gate_pre, approximate=True) * up_proj).astype(jnp.bfloat16)
    down_part = jnp.einsum("bsf,fd->bsd", ffn_act, w_down, preferred_element_type=jnp.float32).astype(jnp.bfloat16)
    down_proj = lax.psum_scatter(down_part, "tp", scatter_dimension=1, tiled=True)
    return (resid_one.astype(jnp.float32) + rms_norm(down_proj, norm_post_ffw).astype(jnp.float32)).astype(jnp.bfloat16)


def solution(mesh):
    in_specs = (P("dp", None), P("dp", None), P("tp", None), P(None, "tp", None), P(None, "tp", None), P(None, "tp", None), P("tp", None, None), P(None, "tp"), P(None, "tp"), P("tp", None), P(None), P(None), P(None), P(None))

    def device_step(tokens, positions, embed_block, w_query, w_key, w_value, w_out, w_gate, w_up, w_down, norm_pre_att, norm_post_att, norm_pre_ffw, norm_post_ffw):
        dev_rank = lax.axis_index("tp")
        vocab_local, model_dim = embed_block.shape
        local_ids = tokens - dev_rank * vocab_local
        in_block = (local_ids >= 0) & (local_ids < vocab_local)
        looked = jnp.take(embed_block, jnp.clip(local_ids, 0, vocab_local - 1), axis=0)
        normalizer = jnp.sqrt(jnp.float32(model_dim)).astype(jnp.bfloat16)
        partial_emb = jnp.where(in_block[:, :, None], looked * normalizer, jnp.zeros((), jnp.bfloat16))
        embeds = lax.psum_scatter(partial_emb, "tp", scatter_dimension=1, tiled=True)
        return decoder_layer(embeds, positions, w_query, w_key, w_value, w_out, w_gate, w_up, w_down, norm_pre_att, norm_post_att, norm_pre_ffw, norm_post_ffw)

    return jax.shard_map(device_step, mesh=mesh, in_specs=in_specs, out_specs=P("dp", "tp", None), check_vma=False)
```

profile of v0, /device:TPU:0, one launch (start us, length us, event | category | flops | bytes accessed | tf_op | source)
XLA Modules:
  0.0 196.8 jit_solution(18222950257165659217)
XLA Ops:
  6.5 0.0 copy-start
  6.5 0.8 and_reduce_fusion
  7.4 6.1 %gather_fusion = bf16[256,3072]{1,0:T(8,128)(2,1)S(1)} fusion(bf16[32064,3072]{1,0:T(8,128)(2,1)} %param.18, s32[1024]{0:T(1024)S(1)} %pad_clamp_fusion), kind=kCustom, calls=%fused_computation | custom fusion | bytes 3146752 | tf_op jit(solution)/shard_map/jit(_take)/gather | solution.py:94
  13.5 0.0 copy-start.9
  13.5 1.5 fusion.45
  15.0 0.0 reduce-scatter.4.cloned.1.call-update
  15.0 0.0 all-gather.3.cloned.1.call-start
  15.1 39.3 %reduce-scatter.4.cloned.1.call-done = bf16[1,64,3072]{2,1,0:T(8,128)(2,1)} async-done(((bf16[1,256,3072]{2,1,0:T(8,128)(2,1)}), bf16[1,64,3072]{2,1,0:T(8,128)(2,1)}) %reduce-scatter.4.cloned.1.call-update) | async-done | bytes 393232 | tf_op jit(solution)/shard_map/reduce_scatter | solution.py:97
  54.4 1.2 fusion.63
  55.6 0.0 copy-start.8
  55.6 1.9 fusion.65
  57.6 0.0 all-gather.3.cloned.1.call-update
  57.6 0.0 reduce-scatter.6.cloned.1.call-start
  57.7 3.6 %copy.25 = bf16[3072,2,128]{0,2,1:T(8,128)(2,1)S(1)} copy(bf16[3072,2,128]{2,1,0:T(2,128)(2,1)} %param.20) | data formatting | bytes 3145728 | tf_op args[4]
  61.2 0.0 copy-done.8
  61.3 6.7 %copy.22 = bf16[3072,6,128]{0,2,1:T(8,128)(2,1)} copy(bf16[3072,6,128]{2,0,1:T(8,128)(2,1)} %param.19) | data formatting | bytes 9437184 | tf_op args[3]
  67.9 0.3 multiply_cosine_fusion
  68.2 0.0 copy-start.3
  68.3 0.0 copy-start.5
  68.3 6.1 %all-gather.3.cloned.1.call-done = bf16[1,256,3072]{2,1,0:T(8,128)(2,1)} async-done(((bf16[1,64,3072]{2,1,0:T(8,128)(2,1)}), bf16[1,256,3072]{2,1,0:T(8,128)(2,1)}) %all-gather.3.cloned.1.call-update) | async-done | bytes 1572880 | tf_op jit(solution)/shard_map/all_gather | solution.py:64
  74.4 2.0 %fusion.40 = f32[256,256]{0,1:S(1)} fusion(bf16[3072,256]{0,1:T(8,128)(2,1)S(1)} %bitcast.120, bf16[1,256,3072]{2,1,0:T(8,128)(2,1)} %all-gather.3.cloned.1.call-done), kind=kOutput, calls=%fused_computation.45 | convolution fusion | flops 402653184 | bytes 3407872
  76.5 0.8 copy.27
  77.2 4.3 %fusion.42 = f32[256,768]{0,1:S(1)} fusion(bf16[3072,768]{0,1:T(8,128)(2,1)} %bitcast.121, bf16[1,256,3072]{2,1,0:T(8,128)(2,1)} %all-gather.3.cloned.1.call-done), kind=kOutput, calls=%fused_computation.47 | convolution fusion | flops 1207959552 | bytes 7077888
  81.5 0.0 copy-done.4
  81.5 0.0 copy-done.6
  81.5 0.1 multiply_subtract_fusion
  81.7 0.3 copy.23
  81.9 0.3 copy.24
  82.2 0.3 fusion.71
  82.5 0.0 copy-start.13
  82.5 2.0 %fusion.52 = bf16[1,256,2,128]{3,1,2,0:T(8,128)(2,1)S(1)} fusion(bf16[3072,2,128]{2,1,0:T(2,128)(2,1)S(1)} %copy-done, bf16[1,256,3072]{2,1,0:T(8,128)(2,1)} %all-gather.3.cloned.1.call-done), kind=kOutput, calls=%fused_computation.60 | convolution fusion | flops 402718720 | bytes 3276800 | tf_op jit(solution)/shard_map/bsd,dnh->bsnh/dot_general | solution.py:71
  84.6 0.0 copy-done.7
  84.6 0.0 copy-done.13
  84.6 5.1 %while.10 = (s32[]{:T(128)}, bf16[2,1,128,2,3,128]{5,2,0,4,3,1:T(8,128)(2,1)S(1)}, s32[2]{0:T(128)S(1)}, s32[1,256]{1,0:T(1,128)S(1)}, bf16[1,256,2,3,128]{4,1,3...) while((s32[]{:T(128)}, ...), condition=%wide.region_5.6_spmd, body=%wide.region_2.5_spmd.sunk | while | flops 102660608 | bytes 3100339 | solution.py:55
  84.6 0.6 dynamic_slice.29
  85.9 0.1 fusion.96
  86.0 0.4 fusion.97
  86.4 0.3 fusion.98
  86.7 0.4 fusion.99
  87.2 0.6 dynamic_slice.29
  88.4 0.1 fusion.96
  88.5 0.4 fusion.97
  88.9 0.3 fusion.98
  89.3 0.4 fusion.99
  89.7 0.0 copy-start.10
  89.7 0.0 copy-start.11
  89.7 4.8 %fusion.23 = bf16[1,256,3072]{2,1,0:T(8,128)(2,1)} fusion(bf16[2,3,128,3072]{3,2,1,0:T(8,128)(2,1)} %bitcast.129, bf16[256,2,3,128]{3,0,2,1:T(8,128)(2,1)S(1)} %bitcast.130), kind=kOutput, calls=%fused_computation.28 | convolution fusion | flops 1208745984 | bytes 6684672 | tf_op jit(solution)/shard_map/bskgh,kghd->bsd/dot_general | solution.py:74
  94.6 0.0 reduce-scatter.6.cloned.1.call-update
  94.6 0.0 all-gather.5.cloned.1.call-start
  94.7 0.0 copy-done.10
  94.7 0.0 copy-done.11
  94.7 22.4 %reduce-scatter.6.cloned.1.call-done = bf16[1,64,3072]{2,1,0:T(8,128)(2,1)} async-done(((bf16[1,256,3072]{2,1,0:T(8,128)(2,1)}), bf16[1,64,3072]{2,1,0:T(8,128)(2,1)}) %reduce-scatter.6.cloned.1.call-update) | async-done | bytes 393232 | tf_op jit(solution)/shard_map/reduce_scatter | solution.py:75
  117.1 1.2 fusion.57
  118.3 1.4 fusion.67
  119.6 0.9 fusion.69
  120.6 0.0 all-gather.5.cloned.1.call-update
  120.6 0.2 reduce-scatter.8.cloned.1.call-start
  120.8 16.6 %all-gather.5.cloned.1.call-done = bf16[1,256,3072]{2,1,0:T(8,128)(2,1)} async-done(((bf16[1,64,3072]{2,1,0:T(8,128)(2,1)}), bf16[1,256,3072]{2,1,0:T(8,128)(2,1)}) %all-gather.5.cloned.1.call-update) | async-done | bytes 1572880 | tf_op jit(solution)/shard_map/all_gather | solution.py:77
  137.4 9.8 %fusion.36 = f32[256,2048]{1,0:T(8,128)} fusion(bf16[3072,2048]{1,0:T(8,128)(2,1)} %param.23, bf16[1,256,3072]{2,1,0:T(8,128)(2,1)} %all-gather.5.cloned.1.call-done), kind=kOutput, calls=%fused_computation.41 | convolution fusion | flops 3221225472 | bytes 16252928 | tf_op jit(solution)/shard_map/bsd,df->bsf/dot_general | solution.py:78
  147.2 17.4 %fusion.26 = bf16[1,256,3072]{2,1,0:T(8,128)(2,1)} fusion(bf16[2048,3072]{1,0:T(8,128)(2,1)} %param.25, bf16[3072,2048]{1,0:T(8,128)(2,1)} %param.24, f32[256,2048]{1,0:T(8,128)} %fusion.36, bf16[1,256,3072]{2,1,0:T(8,128)(2,1)} %all-gather.5.cloned.1.call-done), kind=kOutput, calls=%fused_computation.29 | convolution fusion | flops 6448480256 | bytes 30408704 | tf_op jit(solution)/shard_map/bsf,fd->bsd/dot_general | solution.py:81
  164.6 0.0 reduce-scatter.8.cloned.1.call-update
  164.7 22.5 %reduce-scatter.8.cloned.1.call-done = bf16[1,64,3072]{2,1,0:T(8,128)(2,1)} async-done(((bf16[1,256,3072]{2,1,0:T(8,128)(2,1)}), bf16[1,64,3072]{2,1,0:T(8,128)(2,1)}) %reduce-scatter.8.cloned.1.call-update) | async-done | bytes 393232 | tf_op jit(solution)/shard_map/reduce_scatter | solution.py:82
  187.1 1.2 fusion.60
  188.3 2.0 fusion.70
  (31 shorter events, 0.2 us)
Async XLA Ops:
  6.5 75.9 %copy-start = (bf16[3072,2,128]{2,1,0:T(2,128)(2,1)S(1)}, bf16[3072,2,128]{2,1,0:T(2,128)(2,1)}, u32[]{:S(2)}) copy-start(bf16[3072,2,128]{2,1,0:T(2,128)(2,1)} %param.21) | copy-start | bytes 4718596
  6.5 47.9 %reduce-scatter.4.cloned.1.call-start = ((), (), s32[]{:S(2)}) async-start(), calls=%async_computation.3 | async-start | bytes 1966080 | tf_op jit(solution)/shard_map/reduce_scatter | solution.py:97
  13.5 1.6 copy-start.9
  15.0 59.3 %all-gather.3.cloned.1.call-start = ((), (), s32[]{:S(2)}) async-start(), calls=%async_computation.4 | async-start | bytes 1966080 | tf_op jit(solution)/shard_map/all_gather | solution.py:64
  55.6 5.6 %copy-start.8 = (s32[1,256]{1,0:T(1,128)S(1)}, s32[1,256]{1,0:T(1,128)}, u32[]{:S(2)}) copy-start(s32[1,256]{1,0:T(1,128)} %param.17) | copy-start | bytes 3076
  57.6 59.5 %reduce-scatter.6.cloned.1.call-start = ((), (), s32[]{:S(2)}) async-start(), calls=%async_computation.5 | async-start | bytes 1966080 | tf_op jit(solution)/shard_map/reduce_scatter | solution.py:75
  68.2 8.2 %copy-start.3 = (f32[256,64]{0,1:T(8,128)}, f32[256,64]{0,1:T(8,128)S(1)}, u32[]{:S(2)}) copy-start(f32[256,64]{0,1:T(8,128)S(1)} %get-tuple-element.81) | copy-start | bytes 196612
  68.3 8.2 %copy-start.5 = (f32[256,64]{0,1:T(8,128)}, f32[256,64]{0,1:T(8,128)S(1)}, u32[]{:S(2)}) copy-start(f32[256,64]{0,1:T(8,128)S(1)} %get-tuple-element.82) | copy-start | bytes 196612
  77.2 4.3 %copy-start.4 = (f32[256,64]{0,1:T(8,128)S(1)}, f32[256,64]{0,1:T(8,128)}, u32[]{:S(2)}) copy-start(f32[256,64]{0,1:T(8,128)} %copy-done.3) | copy-start | bytes 196612
  77.2 4.3 %copy-start.6 = (f32[256,64]{0,1:T(8,128)S(1)}, f32[256,64]{0,1:T(8,128)}, u32[]{:S(2)}) copy-start(f32[256,64]{0,1:T(8,128)} %copy-done.5) | copy-start | bytes 196612
  82.5 2.1 %copy-start.7 = (bf16[1,256,2,128]{3,1,2,0:T(8,128)(2,1)S(1)}, bf16[1,256,2,128]{3,1,2,0:T(8,128)(2,1)}, u32[]{:S(2)}) copy-start(bf16[1,256,2,128]{3,1,2,0:T(8,128)(2,1)} %copy.27) | copy-start | bytes 393220
  82.5 2.1 %copy-start.13 = (bf16[2,1,128,2,3,128]{5,2,0,4,3,1:T(8,128)(2,1)S(1)}, bf16[2,1,128,2,3,128]{5,2,0,4,3,1:T(8,128)(2,1)}, u32[]{:S(2)}) copy-start(bf16[2,1,128,2,3,128]{5,2,0,4,3,1:T(8,128)(2,1)} %custom-call.2) | copy-start | bytes 1179652
  89.7 4.9 %copy-start.10 = (f32[3072]{0:T(1024)S(1)}, f32[3072]{0:T(1024)}, u32[]{:S(2)}) copy-start(f32[3072]{0:T(1024)} %param.27) | copy-start | bytes 36868
  89.7 4.9 %copy-start.11 = (f32[3072]{0:T(1024)S(1)}, f32[3072]{0:T(1024)}, u32[]{:S(2)}) copy-start(f32[3072]{0:T(1024)} %param.28) | copy-start | bytes 36868
  94.6 23.7 %copy-start.2 = (bf16[1,64,3072]{2,1,0:T(8,128)(2,1)S(1)}, bf16[1,64,3072]{2,1,0:T(8,128)(2,1)}, u32[]{:S(2)}) copy-start(bf16[1,64,3072]{2,1,0:T(8,128)(2,1)} %reduce-scatter.4.cloned.1.call-done) | copy-start | bytes 1179652
  94.6 42.8 %all-gather.5.cloned.1.call-start = ((), (), s32[]{:S(2)}) async-start(), calls=%async_computation.6 | async-start | bytes 1966080 | tf_op jit(solution)/shard_map/all_gather | solution.py:77
  120.6 66.5 %reduce-scatter.8.cloned.1.call-start = ((), (), s32[]{:S(2)}) async-start(), calls=%async_computation.7 | async-start | bytes 1966080 | tf_op jit(solution)/shard_map/reduce_scatter | solution.py:82
  147.2 17.4 %copy-start.12 = (f32[3072]{0:T(1024)S(1)}, f32[3072]{0:T(1024)}, u32[]{:S(2)}) copy-start(f32[3072]{0:T(1024)} %param.29) | copy-start | bytes 36868
  147.2 43.1 %copy-start.1 = (bf16[3072,2,128]{2,1,0:T(2,128)(2,1)S(1)}, bf16[3072,2,128]{2,1,0:T(2,128)(2,1)}, u32[]{:S(2)}) copy-start(bf16[3072,2,128]{2,1,0:T(2,128)(2,1)} %param.21) | copy-start | bytes 4718596
Sparse Core Ops, SparseCore 0:
  15.2 39.2 reduce-scatter.3
  57.7 16.6 all-gather.2
  94.7 22.3 reduce-scatter.5
  120.7 16.6 all-gather.4
  164.8 22.3 reduce-scatter.7
where the time goes:
time: 198 us; the launch traced here: 197 us
  waiting for transfers between devices  107 us (54%)
  matrix products  42.1 us (21%)
  local copies, waits for them, and re-layouts  18.9 us (10%)
  other arithmetic  13.7 us (7%)
  between operations  13.5 us (7%)
    reduce_scatter x1, waiting for transfers between devices, device_step(): lax.psum_scatter(partial_emb, 'tp', scatter_dimension=1, tiled=True)  39.3 us
    reduce_scatter x1, waiting for transfers between devices, decoder_layer(): lax.psum_scatter(down_part, 'tp', scatter_dimension=1, tiled=True)  22.5 us
    reduce_scatter x1, waiting for transfers between devices, decoder_layer(): att_proj = lax.psum_scatter(att_part, 'tp', scatter_dimension=1, tiled=True)  22.4 us
    dot_general x1, matrix products, decoder_layer(): jnp.einsum('bsf,fd->bsd', ffn_act, w_down, preferred_element_type=jnp.flo...  17.4 us
    all_gather x1, waiting for transfers between devices, decoder_layer(): lax.all_gather(rms_norm(resid_one, norm_pre_ffw), 'tp', axis=1, tiled=True)  16.6 us
    unnamed x30, local copies, waits for them, and re-layouts  10.3 us
    dot_general x1, matrix products, decoder_layer(): jnp.einsum('bsd,df->bsf', mlp_in, w_gate, preferred_element_type=jnp.floa...  9.81 us
    unnamed x2, matrix products  6.28 us
  transfers between devices with their start and end apart: 5, of which 5 were waited for; matrix products, arithmetic and copies ran while one was open for 5% of the time, Pallas kernels for 0%

commit v1 on v0

v1 whole, which is shorter than its diff:
```python
import functools

import jax
import jax.numpy as jnp
import numpy as np
from jax import lax
from jax.experimental import pallas as pl
from jax.experimental.pallas import tpu as pltpu
from jax.sharding import PartitionSpec as P

WINDOW = 4096
QUERY_SCALE = 256.0 ** -0.5
SOFT_CAP = 50.0
NORM_EPS = 1e-6
ROPE_BASE = 10000.0
SEQ = 256
DIM = 3072
FFN = 2048
CHUNK = 128
HALF = 64
ROWP = 16
NRP = HALF // ROWP
COLP = 1024
NCP = DIM // COLP
BF = jnp.bfloat16
F32 = jnp.float32


def rms_rows(u, gain):
    mean_sq = jnp.mean(u * u, axis=-1, keepdims=True)
    return (u * lax.rsqrt(mean_sq + NORM_EPS) * gain).astype(BF)


def layer_kernel(looked, scale_col, cos_tab, sin_tab, pos_col, pos_row, wq_hbm, wk_hbm, wv_hbm, wo_hbm, wg_hbm, wu_hbm, wd_hbm, g1, g2, g3, g4,
                 out,
                 wqkv, wo, wg, wu, wd, part, ssum, rd, rxe, rxy, rxz, act, resid, hid, qs, ks, vs, os_, f32buf,
                 wsem, esend, erecv, exsend, exrecv, asend, arecv, ysend, yrecv, yxsend, yxrecv, msend, mrecv, zsend, zrecv, zxsend, zxrecv):
    tp = lax.axis_index("tp")
    chip = tp // 2
    core = tp % 2
    partner = chip * 2 + (1 - core)
    peer = (1 - chip) * 2 + core

    def remote(src, dst, ssem, rsem, dev):
        return pltpu.make_async_remote_copy(src_ref=src, dst_ref=dst, send_sem=ssem, recv_sem=rsem, device_id={"tp": dev}, device_id_type=pl.DeviceIdType.MESH)

    look_cp = pltpu.make_async_copy(looked, part, wsem.at[0])
    look_cp.start()
    raw_cps = []
    for i in range(3):
        raw_cps.append(pltpu.make_async_copy(wk_hbm.at[pl.ds(2048 * i, 2048)], wd.at[:, pl.ds(128 * i, 128)], wsem.at[1 + i]))
        raw_cps.append(pltpu.make_async_copy(wv_hbm.at[pl.ds(2048 * i, 2048)], wd.at[:, pl.ds(384 + 128 * i, 128)], wsem.at[4 + i]))
    for cp in raw_cps:
        cp.start()
    q_cps = [pltpu.make_async_copy(wq_hbm.at[h], wqkv.at[:, pl.ds(128 * h, 128)], wsem.at[7 + h]) for h in range(6)]
    for cp in q_cps:
        cp.start()
    wo_cp = pltpu.make_async_copy(wo_hbm, wo, wsem.at[13])
    wo_cp.start()
    wg_cp = pltpu.make_async_copy(wg_hbm, wg, wsem.at[14])
    wu_cp = pltpu.make_async_copy(wu_hbm, wu, wsem.at[15])
    wd_cp = pltpu.make_async_copy(wd_hbm, wd, wsem.at[16])
    wg_cp.start()
    wu_cp.start()

    barrier = pltpu.get_barrier_semaphore()
    for dev in (partner, peer):
        pl.semaphore_signal(barrier, inc=1, device_id={"tp": dev}, device_id_type=pl.DeviceIdType.MESH)
    pl.semaphore_wait(barrier, 2)

    def own(k):
        return pl.multiple_of(CHUNK * k + HALF * core, HALF)

    def theirs(k):
        return pl.multiple_of(CHUNK * k + HALF * (1 - core), HALF)

    look_cp.wait()

    def e_d2d(k, j):
        return remote(part.at[pl.ds(theirs(k) + ROWP * j, ROWP)], rd.at[k, pl.ds(ROWP * j, ROWP)], esend.at[k, j], erecv.at[k, j], partner)

    def e_x(k, j):
        sl = pl.ds(ROWP * j, ROWP)
        return remote(ssum.at[k, sl], rxe.at[k, sl], exsend.at[k, j], exrecv.at[k, j], peer)

    def a_d2d(k, j):
        sl = pl.ds(own(k) + ROWP * j, ROWP)
        return remote(act.at[sl], act.at[sl], asend.at[k, j], arecv.at[k, j], partner)

    def a_in(k, j):
        sl = pl.ds(theirs(k) + ROWP * j, ROWP)
        return remote(act.at[sl], act.at[sl], asend.at[k, j], arecv.at[k, j], partner)

    def scale_rows(row):
        sl = pl.ds(row, ROWP)
        part[sl, :] = (part[sl, :].astype(F32) * scale_col[sl, :]).astype(BF)

    for k in range(2):
        for j in range(NRP):
            scale_rows(pl.multiple_of(theirs(k) + ROWP * j, ROWP))
            e_d2d(k, j).start()
        for j in range(NRP):
            scale_rows(pl.multiple_of(own(k) + ROWP * j, ROWP))
    for k in range(2):
        for j in range(NRP):
            sl = pl.ds(ROWP * j, ROWP)
            e_d2d(k, j).wait_recv()
            ssum[k, sl, :] = part[pl.ds(pl.multiple_of(own(k) + ROWP * j, ROWP), ROWP), :] + rd[k, sl, :]
            e_x(k, j).start()

    for cp in raw_cps:
        cp.wait()
    for w in range(2):
        for i in range(3):
            def split_heads(b, carry, w=w, i=i):
                row = pl.multiple_of(b * 512, 512)
                f32buf[...] = wd[pl.ds(row, 512), pl.ds(384 * w + 128 * i, 128)].astype(F32)
                dst = pl.ds(pl.multiple_of(1024 * i + b * 256, 256), 256)
                for h in range(2):
                    wqkv[dst, pl.ds(768 + 256 * w + 128 * h, 128)] = f32buf[pl.ds(h, 256, stride=2), :].astype(BF)
                return carry
            lax.fori_loop(0, 4, split_heads, 0)
    wd_cp.start()

    gain1 = 1.0 + g1[...]
    gain2 = 1.0 + g2[...]
    gain3 = 1.0 + g3[...]
    gain4 = 1.0 + g4[...]

    def embed_chunk(k):
        for j in range(NRP):
            sl = pl.ds(ROWP * j, ROWP)
            e_x(k, j).wait_recv()
            emb = ssum[k, sl, :] + rxe[k, sl, :]
            resid[k, sl, :] = emb
            act[pl.ds(pl.multiple_of(own(k) + ROWP * j, ROWP), ROWP), :] = rms_rows(emb.astype(F32), gain1)
            a_d2d(k, j).start()
        for j in range(NRP):
            a_in(k, j).wait_recv()

    def qkv_chunk(k):
        rows = pl.ds(CHUNK * k, CHUNK)
        cos_c = cos_tab[rows, :]
        sin_c = sin_tab[rows, :]

        def rope(u):
            return u * cos_c + pltpu.roll(u, 64, 1) * sin_c

        for b in range(5):
            prod = jnp.dot(act[rows, :], wqkv[:, pl.ds(256 * b, 256)], preferred_element_type=F32)
            for h in range(2):
                u = prod[:, 128 * h:128 * h + 128]
                if b < 3:
                    qs[2 * b + h] = (rope(u) * QUERY_SCALE).astype(BF)
                elif b == 3:
                    ks[h, rows, :] = rope(u).astype(BF)
                else:
                    vs[h, rows, :] = u.astype(BF)

    def attend_chunk(k):
        span = CHUNK * (k + 1)
        offset = pos_col[pl.ds(CHUNK * k, CHUNK), :] - pos_row[:, pl.ds(0, span)]
        keep = (offset >= 0) & (offset < WINDOW)
        for g in range(2):
            kk = ks[g, pl.ds(0, span), :]
            vv = vs[g, pl.ds(0, span), :]
            for i in range(3):
                s = lax.dot_general(qs[3 * g + i], kk, (((1,), (1,)), ((), ())), preferred_element_type=F32)
                c = SOFT_CAP * jnp.tanh(s * (1.0 / SOFT_CAP))
                e = jnp.where(keep, jnp.exp(c), 0.0)
                pr = (e * (1.0 / jnp.sum(e, axis=-1, keepdims=True))).astype(BF)
                o = jnp.dot(pr, vv, preferred_element_type=F32)
                os_[:, pl.ds(128 * (3 * g + i), 128)] = o.astype(BF)

    def y_d2d(k, n):
        cs = pl.ds(COLP * n, COLP)
        return remote(part.at[pl.ds(theirs(k), HALF), cs], rd.at[k, :, cs], ysend.at[k, n], yrecv.at[k, n], partner)

    def y_x(k, n):
        cs = pl.ds(COLP * n, COLP)
        return remote(ssum.at[k, :, cs], rxy.at[k, :, cs], yxsend.at[k, n], yxrecv.at[k, n], peer)

    def out_chunk(k):
        rows = pl.ds(CHUNK * k, CHUNK)
        for j in range(NRP):
            e_d2d(k, j).wait_send()
        for n in range(NCP):
            def col(b, carry, n=n):
                cs = pl.ds(pl.multiple_of(COLP * n + 256 * b, 256), 256)
                part[rows, cs] = jnp.dot(os_[...], wo[:, cs], preferred_element_type=F32).astype(BF)
                return carry
            lax.fori_loop(0, COLP // 256, col, 0)
            y_d2d(k, n).start()
        for j in range(NRP):
            e_x(k, j).wait_send()
        for n in range(NCP):
            cs = pl.ds(COLP * n, COLP)
            y_d2d(k, n).wait_recv()
            ssum[k, :, cs] = (part[pl.ds(own(k), HALF), cs].astype(F32) + rd[k, :, cs].astype(F32)).astype(BF)
            y_x(k, n).start()

    def mid_chunk(k):
        for j in range(NRP):
            a_d2d(k, j).wait_send()
        for n in range(NCP):
            y_x(k, n).wait_recv()
        for j in range(NRP):
            sl = pl.ds(ROWP * j, ROWP)
            y = (ssum[k, sl, :].astype(F32) + rxy[k, sl, :].astype(F32)).astype(BF).astype(F32)
            x1 = (resid[k, sl, :].astype(F32) + rms_rows(y, gain2).astype(F32)).astype(BF)
            resid[k, sl, :] = x1
            act[pl.ds(pl.multiple_of(own(k) + ROWP * j, ROWP), ROWP), :] = rms_rows(x1.astype(F32), gain3)
            m_d2d(k, j).start()
        for j in range(NRP):
            m_in(k, j).wait_recv()

    def m_d2d(k, j):
        sl = pl.ds(own(k) + ROWP * j, ROWP)
        return remote(act.at[sl], act.at[sl], msend.at[k, j], mrecv.at[k, j], partner)

    def m_in(k, j):
        sl = pl.ds(theirs(k) + ROWP * j, ROWP)
        return remote(act.at[sl], act.at[sl], msend.at[k, j], mrecv.at[k, j], partner)

    def z_d2d(k, n):
        cs = pl.ds(COLP * n, COLP)
        return remote(part.at[pl.ds(theirs(k), HALF), cs], rd.at[k, :, cs], zsend.at[k, n], zrecv.at[k, n], partner)

    def z_x(k, n):
        cs = pl.ds(COLP * n, COLP)
        return remote(ssum.at[k, :, cs], rxz.at[:, cs], zxsend.at[n], zxrecv.at[n], peer)

    def ffn_chunk(k):
        rows = pl.ds(CHUNK * k, CHUNK)

        def up(b, carry):
            cs = pl.ds(pl.multiple_of(256 * b, 256), 256)
            gate = jnp.dot(act[rows, :], wg[:, cs], preferred_element_type=F32)
            upp = jnp.dot(act[rows, :], wu[:, cs], preferred_element_type=F32)
            hid[:, cs] = (jax.nn.gelu(gate, approximate=True) * upp).astype(BF)
            return carry
        lax.fori_loop(0, FFN // 256, up, 0)
        for n in range(NCP):
            y_d2d(k, n).wait_send()
        if k == 0:
            wd_cp.wait()
        for n in range(NCP):
            def col(b, carry, n=n):
                cs = pl.ds(pl.multiple_of(COLP * n + 256 * b, 256), 256)
                part[rows, cs] = jnp.dot(hid[...], wd[:, cs], preferred_element_type=F32).astype(BF)
                return carry
            lax.fori_loop(0, COLP // 256, col, 0)
            z_d2d(k, n).start()
        for n in range(NCP):
            y_x(k, n).wait_send()
        for n in range(NCP):
            cs = pl.ds(COLP * n, COLP)
            z_d2d(k, n).wait_recv()
            ssum[k, :, cs] = (part[pl.ds(own(k), HALF), cs].astype(F32) + rd[k, :, cs].astype(F32)).astype(BF)

            @pl.when(chip != k)
            def _(k=k, n=n):
                z_x(k, n).start()

    embed_chunk(0)
    for cp in q_cps:
        cp.wait()
    qkv_chunk(0)
    attend_chunk(0)
    wo_cp.wait()
    out_chunk(0)
    embed_chunk(1)
    qkv_chunk(1)
    attend_chunk(1)
    out_chunk(1)
    mid_chunk(0)
    wg_cp.wait()
    wu_cp.wait()
    ffn_chunk(0)
    mid_chunk(1)
    ffn_chunk(1)
    for n in range(NCP):
        z_x(0, n).wait_recv()
    for j in range(NRP):
        sl = pl.ds(ROWP * j, ROWP)
        z = (ssum[chip, sl, :].astype(F32) + rxz[sl, :].astype(F32)).astype(BF).astype(F32)
        out[0, sl, :] = (resid[chip, sl, :].astype(F32) + rms_rows(z, gain4).astype(F32)).astype(BF)
    for k in range(2):
        for j in range(NRP):
            m_d2d(k, j).wait_send()
        for n in range(NCP):
            z_d2d(k, n).wait_send()
    for n in range(NCP):
        z_x(0, n).wait_send()


def solution(mesh):
    in_specs = (P("dp", None), P("dp", None), P("tp", None), P(None, "tp", None), P(None, "tp", None), P(None, "tp", None), P("tp", None, None), P(None, "tp"), P(None, "tp"), P("tp", None), P(None), P(None), P(None), P(None))

    vm = pl.BlockSpec(memory_space=pltpu.VMEM)
    hb = pl.BlockSpec(memory_space=pl.ANY)
    dma = pltpu.SemaphoreType.DMA
    kernel = pl.pallas_call(
        layer_kernel,
        out_shape=jax.ShapeDtypeStruct((1, HALF, DIM), BF),
        in_specs=[hb, vm, vm, vm, vm, vm] + [hb] * 7 + [vm] * 4,
        out_specs=vm,
        scratch_shapes=[
            pltpu.VMEM((DIM, 1280), BF),
            pltpu.VMEM((768, DIM), BF),
            pltpu.VMEM((DIM, FFN), BF),
            pltpu.VMEM((DIM, FFN), BF),
            pltpu.VMEM((FFN, DIM), BF),
            pltpu.VMEM((SEQ, DIM), BF),
            pltpu.VMEM((2, HALF, DIM), BF),
            pltpu.VMEM((2, HALF, DIM), BF),
            pltpu.VMEM((2, HALF, DIM), BF),
            pltpu.VMEM((2, HALF, DIM), BF),
            pltpu.VMEM((HALF, DIM), BF),
            pltpu.VMEM((SEQ, DIM), BF),
            pltpu.VMEM((2, HALF, DIM), BF),
            pltpu.VMEM((CHUNK, FFN), BF),
            pltpu.VMEM((6, CHUNK, 128), BF),
            pltpu.VMEM((2, SEQ, 128), BF),
            pltpu.VMEM((2, SEQ, 128), BF),
            pltpu.VMEM((CHUNK, 768), BF),
            pltpu.VMEM((512, 128), F32),
            dma((17,)),
            dma((2, NRP)), dma((2, NRP)),
            dma((2, NRP)), dma((2, NRP)),
            dma((2, NRP)), dma((2, NRP)),
            dma((2, NCP)), dma((2, NCP)),
            dma((2, NCP)), dma((2, NCP)),
            dma((2, NRP)), dma((2, NRP)),
            dma((2, NCP)), dma((2, NCP)),
            dma((NCP,)), dma((NCP,)),
        ],
        compiler_params=pltpu.CompilerParams(collective_id=0, has_side_effects=True, vmem_limit_bytes=67043328),
        name="decoder_layer",
    )

    def device_step(tokens, positions, embed_block, w_query, w_key, w_value, w_out, w_gate, w_up, w_down, g1, g2, g3, g4):
        dev_rank = lax.axis_index("tp")
        vocab_local, model_dim = embed_block.shape
        ids = tokens[0] - dev_rank * vocab_local
        in_block = (ids >= 0) & (ids < vocab_local)
        looked = jnp.take(embed_block, jnp.clip(ids, 0, vocab_local - 1), axis=0, mode="clip")
        normalizer = float(np.asarray(np.sqrt(np.float32(model_dim)), dtype=jnp.bfloat16))
        scale_col = jnp.where(in_block, jnp.float32(normalizer), jnp.float32(0.0))[:, None]
        inv_freq = ROPE_BASE ** (-2.0 * jnp.arange(64, dtype=F32) / 128)
        angles = positions[0].astype(F32)[:, None] * inv_freq
        cos_h, sin_h = jnp.cos(angles), jnp.sin(angles)
        cos_tab = jnp.concatenate([cos_h, cos_h], axis=1)
        sin_tab = jnp.concatenate([-sin_h, sin_h], axis=1)
        return kernel(looked, scale_col, cos_tab, sin_tab, positions.reshape(SEQ, 1), positions,
                      w_query.transpose(1, 0, 2), w_key.reshape(2 * model_dim, 128), w_value.reshape(2 * model_dim, 128), w_out.reshape(768, model_dim),
                      w_gate, w_up, w_down, g1[None], g2[None], g3[None], g4[None])

    return jax.shard_map(device_step, mesh=mesh, in_specs=in_specs, out_specs=P("dp", "tp", None), check_vma=False)
```

time: 198 us -> 97.8 us (0.49)
  waiting for transfers between devices: 107 us -> 0 us
  Pallas kernels: 0 us -> 82.9 us
  matrix products: 42.1 us -> 0 us
  between operations: 13.5 us -> 0.02 us
  other arithmetic: 13.7 us -> 3.45 us
  local copies, waits for them, and re-layouts: 18.9 us -> 11.2 us
    reduce_scatter x3 -> x0, waiting for transfers between devices: 84.2 us -> none  [the longest x1 39.3 us: device_step(): lax.psum_scatter(partial_emb, 'tp', scatter_dimension=1, tiled=True)]
    pallas_call x0 -> x1, Pallas kernels: none -> 82.9 us  [device_step(): kernel(looked, scale_col, cos_tab, sin_tab, positions.reshape(SEQ, 1), po...]
    dot_general x8 -> x0, matrix products: 35.8 us -> none  [the longest x1 17.4 us: decoder_layer(): jnp.einsum('bsf,fd->bsd', ffn_act, w_down, preferred_element_type=jnp.flo...]
    all_gather x2 -> x0, waiting for transfers between devices: 22.7 us -> none  [the longest x1 16.6 us: decoder_layer(): lax.all_gather(rms_norm(resid_one, norm_pre_ffw), 'tp', axis=1, tiled=True)]
    unnamed x30 -> x1, local copies, waits for them, and re-layouts: 10.3 us -> 1.77 us
    unnamed x2 -> x0, matrix products: 6.28 us -> none
    reduce_sum x6 -> x0, other arithmetic: 5.53 us -> none  [the longest x4 4.88 us: rms_norm(): mean_sq = jnp.mean(hidden * hidden, axis=-1, keepdims=True)]
    convert_element_type x5 -> x1, other arithmetic: 5.08 us -> 0.68 us  [device_step(): angles = positions[0].astype(F32)[:, None] * inv_freq]
  transfers between devices with their start and end apart: 5 -> 0, of which waited for: 5 -> 0; matrix products, arithmetic and copies ran while one was open for 5% -> 0% of each run, Pallas kernels for 0% -> 0%
where the time goes in v1:
time: 97.8 us; the launch traced here: 97.5 us
  Pallas kernels  82.9 us (85%)
  local copies, waits for them, and re-layouts  11.2 us (11%)
  other arithmetic  3.45 us (4%)
    pallas_call x1, Pallas kernels, device_step(): kernel(looked, scale_col, cos_tab, sin_tab, positions.reshape(SEQ, 1), po...  82.9 us
    gather x1, local copies, waits for them, and re-layouts, device_step(): jnp.take(embed_block, jnp.clip(ids, 0, vocab_local - 1), axis=0, mode='cl...  7.16 us

profile of v1, /device:TPU:0, one launch (start us, length us, event | category | flops | bytes accessed | tf_op | source)
XLA Modules:
  0.0 97.5 jit_solution(11064843189527322353)
XLA Ops:
  0.0 0.7 fusion.1
  0.7 0.7 subtract_clamp_fusion
  1.4 0.7 convert_element_type.10
  2.1 0.8 copy.15.scale_col
  2.9 1.5 %copy.16.pos_col = s32[256,1]{1,0:T(8,128)} copy(s32[256,1]{0,1:T(1,128)} %bitcast.21) | data formatting | bytes 2048 | tf_op jit(solution)/shard_map/squeeze | solution.py:351
  4.3 0.5 fusion
  4.9 0.8 pad_maximum_fusion
  5.7 7.2 %gather_fusion = bf16[256,3072]{1,0:T(8,128)(2,1)} fusion(bf16[32064,3072]{1,0:T(8,128)(2,1)} %param.16, s32[1024]{0:T(1024)S(1)} %pad_clamp_fusion), kind=kCustom, calls=%fused_computation | custom fusion | bytes 3146752 | tf_op jit(solution)/shard_map/jit(_take)/gather | solution.py:347
  12.9 82.9 %decoder_layer.1 = bf16[1,64,3072]{2,1,0:T(8,128)(2,1)} custom-call(bf16[256,3072]{1,0:T(8,128)(2,1)} %gather_fusion, f32[256,1]{1,0:T(8,128)} %copy.15.scale_col, f32[256,128]{1,0:T(8,128)} %get-tuple-element.8.cos_tab, f32[256,128]{1,0:T(8,128)} %get-tuple-element.9.sin_tab, s32[256,1]{1,0:T(8,128)} %copy.16.pos_col, s32[1,256]{1,0:T(1,128)} %pos_row.1, ...), custom_call_target="tpu_custom_call" | custom-call | tf_op jit(solution)/shard_map/decoder_layer/pallas_call | solution.py:355
  95.8 1.8 %copy.18 = bf16[1,64,3072]{2,1,0:T(8,128)(2,1)} copy(bf16[1,64,3072]{2,1,0:T(8,128)(2,1)} %decoder_layer.1) | data formatting | bytes 786432
  (2 shorter events, 0.0 us)

commit v2 on v1

v2 whole, which is shorter than its diff:
```python
import functools

import jax
import jax.numpy as jnp
import numpy as np
from jax import lax
from jax.experimental import pallas as pl
from jax.experimental.pallas import tpu as pltpu
from jax.sharding import PartitionSpec as P

WINDOW = 4096
QUERY_SCALE = 256.0 ** -0.5
SOFT_CAP = 50.0
NORM_EPS = 1e-6
ROPE_BASE = 10000.0
SEQ = 256
DIM = 3072
FFN = 2048
CHUNK = 128
HALF = 64
QTR = 32
UPB = 512
VOCAB_LOCAL = 32064
NORMALIZER = float(np.asarray(np.sqrt(np.float32(DIM)), dtype=jnp.bfloat16))
ROWP = 16
NRP = HALF // ROWP
COLP = 1024
NCP = DIM // COLP
BF = jnp.bfloat16
F32 = jnp.float32


def rms_rows(u, gain):
    mean_sq = jnp.mean(u * u, axis=-1, keepdims=True)
    return (u * lax.rsqrt(mean_sq + NORM_EPS) * gain).astype(BF)


def column_of(row_f32):
    diag = lax.broadcasted_iota(jnp.int32, (128, 128), 0) == lax.broadcasted_iota(jnp.int32, (128, 128), 1)
    return jnp.sum(jnp.where(diag, jnp.broadcast_to(row_f32, (128, 128)), 0.0), axis=1, keepdims=True)


def layer_kernel(looked, tok_row, pos_row, cos_tab, sin_tab, wq_hbm, wk_hbm, wv_hbm, wo_hbm, wg_hbm, wu_hbm, wd_hbm, g1, g2, g3, g4,
                 out,
                 wqkv, wo, wg, wu, wd, part, ssum, rd, rxe, rxy, rxz, act, resid, hid, qs, ks, vs, os_, f32buf, scale_col, pos_col,
                 wsem, esend, erecv, exsend, exrecv, asend, arecv, ysend, yrecv, yxsend, yxrecv, msend, mrecv, zsend, zrecv, zxsend, zxrecv):
    tp = lax.axis_index("tp")
    chip = tp // 2
    core = tp % 2
    partner = chip * 2 + (1 - core)
    peer = (1 - chip) * 2 + core

    def remote(src, dst, ssem, rsem, dev):
        return pltpu.make_async_remote_copy(src_ref=src, dst_ref=dst, send_sem=ssem, recv_sem=rsem, device_id={"tp": dev}, device_id_type=pl.DeviceIdType.MESH)

    barrier = pltpu.get_barrier_semaphore()
    for dev in (partner, peer):
        pl.semaphore_signal(barrier, inc=1, device_id={"tp": dev}, device_id_type=pl.DeviceIdType.MESH)

    look_cp = pltpu.make_async_copy(looked, part, wsem.at[0])
    look_cp.start()
    raw_cps = []
    for i in range(3):
        raw_cps.append(pltpu.make_async_copy(wk_hbm.at[pl.ds(2048 * i, 2048)], wd.at[:, pl.ds(128 * i, 128)], wsem.at[1 + i]))
        raw_cps.append(pltpu.make_async_copy(wv_hbm.at[pl.ds(2048 * i, 2048)], wd.at[:, pl.ds(384 + 128 * i, 128)], wsem.at[4 + i]))
    for cp in raw_cps:
        cp.start()
    q_cps = [pltpu.make_async_copy(wq_hbm.at[h], wqkv.at[:, pl.ds(128 * h, 128)], wsem.at[7 + h]) for h in range(6)]
    for cp in q_cps:
        cp.start()
    wo_cp = pltpu.make_async_copy(wo_hbm, wo, wsem.at[13])
    wo_cp.start()
    wg_cp = pltpu.make_async_copy(wg_hbm, wg, wsem.at[14])
    wu_cp = pltpu.make_async_copy(wu_hbm, wu, wsem.at[15])
    wd_cp = pltpu.make_async_copy(wd_hbm, wd, wsem.at[16])
    wg_cp.start()
    wu_cp.start()

    ids = tok_row[...] - tp * VOCAB_LOCAL
    scale = jnp.where((ids >= 0) & (ids < VOCAB_LOCAL), NORMALIZER, 0.0).astype(F32)
    pos = pos_row[...]
    pos_hi = (pos >> 16).astype(F32)
    pos_lo = (pos & 65535).astype(F32)
    for k in range(2):
        cs = slice(128 * k, 128 * k + 128)
        scale_col[cs, :] = column_of(scale[:, cs])
        pos_col[cs, :] = column_of(pos_hi[:, cs]).astype(jnp.int32) * 65536 + column_of(pos_lo[:, cs]).astype(jnp.int32)

    def own(k):
        return pl.multiple_of(CHUNK * k + HALF * core, HALF)

    def theirs(k):
        return pl.multiple_of(CHUNK * k + HALF * (1 - core), HALF)

    def mine(f, k):
        return pl.multiple_of(CHUNK * f + HALF * k + QTR * core, QTR)

    def other(f, k):
        return pl.multiple_of(CHUNK * f + HALF * k + QTR * (1 - core), QTR)

    def e_d2d(k, j):
        return remote(part.at[pl.ds(theirs(k) + ROWP * j, ROWP)], rd.at[k, pl.ds(ROWP * j, ROWP)], esend.at[k, j], erecv.at[k, j], partner)

    def e_x(k, j):
        sl = pl.ds(ROWP * j, ROWP)
        return remote(ssum.at[k, sl], rxe.at[k, sl], exsend.at[k, j], exrecv.at[k, j], peer)

    def a_d2d(k, j):
        sl = pl.ds(own(k) + ROWP * j, ROWP)
        return remote(act.at[sl], act.at[sl], asend.at[k, j], arecv.at[k, j], partner)

    def a_in(k, j):
        sl = pl.ds(theirs(k) + ROWP * j, ROWP)
        return remote(act.at[sl], act.at[sl], asend.at[k, j], arecv.at[k, j], partner)

    def y_d2d(k, n):
        cs = pl.ds(COLP * n, COLP)
        return remote(part.at[pl.ds(theirs(k), HALF), cs], rd.at[k, :, cs], ysend.at[k, n], yrecv.at[k, n], partner)

    def y_x(k, f, n):
        sl, cs = pl.ds(QTR * f, QTR), pl.ds(COLP * n, COLP)
        return remote(ssum.at[k, sl, cs], rxy.at[k, sl, cs], yxsend.at[k, f, n], yxrecv.at[k, f, n], peer)

    def m_d2d(k, f, j):
        sl = pl.ds(mine(f, k) + ROWP * j, ROWP)
        return remote(act.at[sl], act.at[sl], msend.at[k, f, j], mrecv.at[k, f, j], partner)

    def m_in(k, f, j):
        sl = pl.ds(other(f, k) + ROWP * j, ROWP)
        return remote(act.at[sl], act.at[sl], msend.at[k, f, j], mrecv.at[k, f, j], partner)

    def z_d2d(f, k, n):
        cs = pl.ds(COLP * n, COLP)
        return remote(part.at[pl.ds(other(f, k), QTR), cs], rd.at[f, pl.ds(QTR * k, QTR), cs], zsend.at[f, k, n], zrecv.at[f, k, n], partner)

    def z_x(f, n):
        cs = pl.ds(COLP * n, COLP)
        return remote(ssum.at[f, pl.ds(pl.multiple_of(QTR * (1 - chip), QTR), QTR), cs], rxz.at[f, :, cs], zxsend.at[f, n], zxrecv.at[f, n], peer)

    def scale_rows(row):
        sl = pl.ds(row, ROWP)
        part[sl, :] = (part[sl, :].astype(F32) * scale_col[sl, :]).astype(BF)

    look_cp.wait()
    pl.semaphore_wait(barrier, 2)
    for k in range(2):
        for j in range(NRP):
            scale_rows(pl.multiple_of(theirs(k) + ROWP * j, ROWP))
            e_d2d(k, j).start()
    for k in range(2):
        for j in range(NRP):
            sl = pl.ds(ROWP * j, ROWP)
            row = pl.multiple_of(own(k) + ROWP * j, ROWP)
            scale_rows(row)
            e_d2d(k, j).wait_recv()
            ssum[k, sl, :] = part[pl.ds(row, ROWP), :] + rd[k, sl, :]
            e_x(k, j).start()

    for cp in raw_cps:
        cp.wait()
    for w in range(2):
        for i in range(3):
            def split_heads(b, carry, w=w, i=i):
                row = pl.multiple_of(b * 512, 512)
                f32buf[...] = wd[pl.ds(row, 512), pl.ds(384 * w + 128 * i, 128)].astype(F32)
                dst = pl.ds(pl.multiple_of(1024 * i + b * 256, 256), 256)
                for h in range(2):
                    wqkv[dst, pl.ds(768 + 256 * w + 128 * h, 128)] = f32buf[pl.ds(h, 256, stride=2), :].astype(BF)
                return carry
            lax.fori_loop(0, 4, split_heads, 0)
    wd_cp.start()

    gain1 = 1.0 + g1[...]
    gain2 = 1.0 + g2[...]
    gain3 = 1.0 + g3[...]
    gain4 = 1.0 + g4[...]

    def embed_chunk(k):
        for j in range(NRP):
            sl = pl.ds(ROWP * j, ROWP)
            e_x(k, j).wait_recv()
            emb = ssum[k, sl, :] + rxe[k, sl, :]
            resid[k, sl, :] = emb
            act[pl.ds(pl.multiple_of(own(k) + ROWP * j, ROWP), ROWP), :] = rms_rows(emb.astype(F32), gain1)
            a_d2d(k, j).start()
        for j in range(NRP):
            a_in(k, j).wait_recv()

    def qkv_chunk(k):
        rows = pl.ds(CHUNK * k, CHUNK)
        cos_c = cos_tab[rows, :]
        sin_c = sin_tab[rows, :]

        def rope(u):
            return u * cos_c + pltpu.roll(u, 64, 1) * sin_c

        for b in range(5):
            prod = jnp.dot(act[rows, :], wqkv[:, pl.ds(256 * b, 256)], preferred_element_type=F32)
            for h in range(2):
                u = prod[:, 128 * h:128 * h + 128]
                if b < 3:
                    qs[2 * b + h] = (rope(u) * QUERY_SCALE).astype(BF)
                elif b == 3:
                    ks[h, rows, :] = rope(u).astype(BF)
                else:
                    vs[h, rows, :] = u.astype(BF)

    def attend_chunk(k):
        span = CHUNK * (k + 1)
        offset = pos_col[pl.ds(CHUNK * k, CHUNK), :] - pos_row[:, pl.ds(0, span)]
        keep = (offset >= 0) & (offset < WINDOW)
        for g in range(2):
            kk = ks[g, pl.ds(0, span), :]
            vv = vs[g, pl.ds(0, span), :]
            for i in range(3):
                s = lax.dot_general(qs[3 * g + i], kk, (((1,), (1,)), ((), ())), preferred_element_type=F32)
                c = SOFT_CAP * jnp.tanh(s * (1.0 / SOFT_CAP))
                e = jnp.where(keep, jnp.exp(c), 0.0)
                pr = (e * (1.0 / jnp.sum(e, axis=-1, keepdims=True))).astype(BF)
                o = jnp.dot(pr, vv, preferred_element_type=F32)
                os_[:, pl.ds(128 * (3 * g + i), 128)] = o.astype(BF)

    def out_chunk(k):
        rows = pl.ds(CHUNK * k, CHUNK)
        for j in range(NRP):
            e_d2d(k, j).wait_send()
            e_x(k, j).wait_send()
            a_d2d(k, j).wait_send()

        def finish(n):
            cs = pl.ds(COLP * n, COLP)
            y_d2d(k, n).wait_recv()
            ssum[k, :, cs] = (part[pl.ds(own(k), HALF), cs].astype(F32) + rd[k, :, cs].astype(F32)).astype(BF)
            y_x(k, 0, n).start()

        for n in range(NCP):
            cs = pl.ds(COLP * n, COLP)
            part[rows, cs] = jnp.dot(os_[...], wo[:, cs], preferred_element_type=F32).astype(BF)
            y_d2d(k, n).start()
            if n > 0:
                finish(n - 1)
        finish(NCP - 1)
        for n in range(NCP):
            y_x(k, 1, n).start()

    def mid_block(k, f):
        for n in range(NCP):
            y_x(k, f, n).wait_recv()
        for j in range(QTR // ROWP):
            sl = pl.ds(QTR * f + ROWP * j, ROWP)
            y = (ssum[k, sl, :].astype(F32) + rxy[k, sl, :].astype(F32)).astype(BF).astype(F32)
            x1 = (resid[k, sl, :].astype(F32) + rms_rows(y, gain2).astype(F32)).astype(BF)
            resid[k, sl, :] = x1
            act[pl.ds(pl.multiple_of(mine(f, k) + ROWP * j, ROWP), ROWP), :] = rms_rows(x1.astype(F32), gain3)
            m_d2d(k, f, j).start()

    def mid_arrive(f):
        for k in range(2):
            for j in range(QTR // ROWP):
                m_in(k, f, j).wait_recv()

    def up_part(f, lo, hi):
        rows = pl.ds(CHUNK * f, CHUNK)

        def up(b, carry):
            cs = pl.ds(pl.multiple_of(UPB * b, UPB), UPB)
            gate = jnp.dot(act[rows, :], wg[:, cs], preferred_element_type=F32)
            upp = jnp.dot(act[rows, :], wu[:, cs], preferred_element_type=F32)
            hid[:, cs] = (jax.nn.gelu(gate, approximate=True) * upp).astype(BF)
            return carry
        lax.fori_loop(lo, hi, up, 0)

    def z_finish(f, n):
        cs = pl.ds(COLP * n, COLP)
        for k in range(2):
            z_d2d(f, k, n).wait_recv()
            sl = pl.ds(QTR * k, QTR)
            ssum[f, sl, cs] = (part[pl.ds(mine(f, k), QTR), cs].astype(F32) + rd[f, sl, cs].astype(F32)).astype(BF)
        z_x(f, n).start()

    def down_part(f):
        rows = pl.ds(CHUNK * f, CHUNK)
        for n in range(NCP):
            cs = pl.ds(COLP * n, COLP)
            part[rows, cs] = jnp.dot(hid[...], wd[:, cs], preferred_element_type=F32).astype(BF)
            for k in range(2):
                z_d2d(f, k, n).start()
            if n > 0:
                z_finish(f, n - 1)

    def output_rows(f):
        for n in range(NCP):
            z_x(f, n).wait_recv()
        keep_row = pl.multiple_of(QTR * chip, QTR)
        for j in range(QTR // ROWP):
            z = (ssum[f, pl.ds(keep_row + ROWP * j, ROWP), :].astype(F32) + rxz[f, pl.ds(ROWP * j, ROWP), :].astype(F32)).astype(BF).astype(F32)
            sl = pl.ds(QTR * f + ROWP * j, ROWP)
            out[0, sl, :] = (resid[chip, sl, :].astype(F32) + rms_rows(z, gain4).astype(F32)).astype(BF)

    embed_chunk(0)
    for cp in q_cps:
        cp.wait()
    qkv_chunk(0)
    attend_chunk(0)
    wo_cp.wait()
    out_chunk(0)
    embed_chunk(1)
    qkv_chunk(1)
    attend_chunk(1)
    out_chunk(1)
    mid_block(0, 0)
    mid_block(0, 1)
    wg_cp.wait()
    wu_cp.wait()
    wd_cp.wait()
    mid_block(1, 0)
    mid_arrive(0)
    up_part(0, 0, FFN // UPB)
    mid_block(1, 1)
    for k in range(2):
        for n in range(NCP):
            y_d2d(k, n).wait_send()
            for f in range(2):
                y_x(k, f, n).wait_send()
    down_part(0)
    mid_arrive(1)
    up_part(1, 0, 1)
    z_finish(0, NCP - 1)
    up_part(1, 1, FFN // UPB)
    down_part(1)
    z_finish(1, NCP - 1)
    output_rows(0)
    output_rows(1)
    for f in range(2):
        for k in range(2):
            for j in range(QTR // ROWP):
                m_d2d(k, f, j).wait_send()
            for n in range(NCP):
                z_d2d(f, k, n).wait_send()
        for n in range(NCP):
            z_x(f, n).wait_send()


def solution(mesh):
    in_specs = (P("dp", None), P("dp", None), P("tp", None), P(None, "tp", None), P(None, "tp", None), P(None, "tp", None), P("tp", None, None), P(None, "tp"), P(None, "tp"), P("tp", None), P(None), P(None), P(None), P(None))

    vm = pl.BlockSpec(memory_space=pltpu.VMEM)
    hb = pl.BlockSpec(memory_space=pl.ANY)
    dma = pltpu.SemaphoreType.DMA
    kernel = pl.pallas_call(
        layer_kernel,
        out_shape=jax.ShapeDtypeStruct((1, HALF, DIM), BF),
        in_specs=[hb, vm, vm, vm, vm] + [hb] * 7 + [vm] * 4,
        out_specs=vm,
        scratch_shapes=[
            pltpu.VMEM((DIM, 1280), BF),
            pltpu.VMEM((768, DIM), BF),
            pltpu.VMEM((DIM, FFN), BF),
            pltpu.VMEM((DIM, FFN), BF),
            pltpu.VMEM((FFN, DIM), BF),
            pltpu.VMEM((SEQ, DIM), BF),
            pltpu.VMEM((2, HALF, DIM), BF),
            pltpu.VMEM((2, HALF, DIM), BF),
            pltpu.VMEM((2, HALF, DIM), BF),
            pltpu.VMEM((2, HALF, DIM), BF),
            pltpu.VMEM((2, QTR, DIM), BF),
            pltpu.VMEM((SEQ, DIM), BF),
            pltpu.VMEM((2, HALF, DIM), BF),
            pltpu.VMEM((CHUNK, FFN), BF),
            pltpu.VMEM((6, CHUNK, 128), BF),
            pltpu.VMEM((2, SEQ, 128), BF),
            pltpu.VMEM((2, SEQ, 128), BF),
            pltpu.VMEM((CHUNK, 768), BF),
            pltpu.VMEM((512, 128), F32),
            pltpu.VMEM((SEQ, 1), F32),
            pltpu.VMEM((SEQ, 1), jnp.int32),
            dma((17,)),
            dma((2, NRP)), dma((2, NRP)),
            dma((2, NRP)), dma((2, NRP)),
            dma((2, NRP)), dma((2, NRP)),
            dma((2, NCP)), dma((2, NCP)),
            dma((2, 2, NCP)), dma((2, 2, NCP)),
            dma((2, 2, QTR // ROWP)), dma((2, 2, QTR // ROWP)),
            dma((2, 2, NCP)), dma((2, 2, NCP)),
            dma((2, NCP)), dma((2, NCP)),
        ],
        compiler_params=pltpu.CompilerParams(collective_id=0, has_side_effects=True, vmem_limit_bytes=67043328),
        name="decoder_layer",
    )

    def device_step(tokens, positions, embed_block, w_query, w_key, w_value, w_out, w_gate, w_up, w_down, g1, g2, g3, g4):
        dev_rank = lax.axis_index("tp")
        vocab_local, model_dim = embed_block.shape
        ids = tokens[0] - dev_rank * vocab_local
        in_block = (ids >= 0) & (ids < vocab_local)
        spread = jnp.arange(SEQ, dtype=jnp.int32) * (vocab_local // SEQ)
        looked = jnp.take(embed_block, jnp.where(in_block, ids, spread), axis=0, mode="clip")
        half = jnp.arange(128, dtype=jnp.int32) % 64
        inv_freq = ROPE_BASE ** (-2.0 * half.astype(F32) / 128)
        angles = positions[0].astype(F32)[:, None] * inv_freq
        cos_tab = jnp.cos(angles)
        sin_tab = jnp.sin(angles) * jnp.where(jnp.arange(128) < 64, -1.0, 1.0).astype(F32)
        return kernel(looked, tokens, positions, cos_tab, sin_tab,
                      w_query.transpose(1, 0, 2), w_key.reshape(2 * model_dim, 128), w_value.reshape(2 * model_dim, 128), w_out.reshape(768, model_dim),
                      w_gate, w_up, w_down, g1[None], g2[None], g3[None], g4[None])

    return jax.shard_map(device_step, mesh=mesh, in_specs=in_specs, out_specs=P("dp", "tp", None), check_vma=False)
```

time: 97.8 us -> 71.8 us (0.73)
  Pallas kernels: 82.9 us -> 61.1 us
  local copies, waits for them, and re-layouts: 11.2 us -> 7.79 us
    pallas_call x1, Pallas kernels: 82.9 us -> 61.1 us  [device_step(): kernel(looked, tokens, positions, cos_tab, sin_tab, w_query.transpose(1,...]
    squeeze x1 -> x0, local copies, waits for them, and re-layouts: 1.47 us -> none  [device_step(): angles = positions[0].astype(F32)[:, None] * inv_freq]
    mul x0 -> x1, other arithmetic: none -> 1.24 us  [device_step(): jnp.sin(angles) * jnp.where(jnp.arange(128) < 64, -1.0, 1.0).astype(F32)]
    gather x1, local copies, waits for them, and re-layouts: 7.16 us -> 6.03 us  [device_step(): jnp.take(embed_block, jnp.where(in_block, ids, spread), axis=0, mode='clip')]
where the time goes in v2:
time: 71.8 us; the launch traced here: 71.5 us
  Pallas kernels  61.1 us (85%)
  local copies, waits for them, and re-layouts  7.79 us (11%)
  other arithmetic  2.62 us (4%)
    pallas_call x1, Pallas kernels, device_step(): kernel(looked, tokens, positions, cos_tab, sin_tab, w_query.transpose(1,...  61.1 us
    gather x1, local copies, waits for them, and re-layouts, device_step(): jnp.take(embed_block, jnp.where(in_block, ids, spread), axis=0, mode='clip')  6.03 us
    unnamed x1, local copies, waits for them, and re-layouts  1.77 us

profile of v2, /device:TPU:0, one launch (start us, length us, event | category | flops | bytes accessed | tf_op | source)
XLA Modules:
  0.0 71.5 jit_solution(1895158009979433839)
XLA Ops:
  0.0 0.7 and_select_fusion
  0.7 0.7 convert_element_type.17
  1.4 1.2 %fusion = (f32[256,128]{1,0:T(8,128)}, f32[256,128]{1,0:T(8,128)}) fusion(f32[128]{0:T(128)S(1)} %get-tuple-element.7, f32[128]{0:T(128)S(1)} %get-tuple-element.8, f32[256]{0:T(256)S(1)} %bitcast.20), kind=kLoop, calls=%fused_computation.3 | loop fusion | flops 65536 | bytes 264192 | tf_op jit(solution)/shard_map/mul | solution.py:402
  2.6 6.0 %gather_fusion = bf16[256,3072]{1,0:T(8,128)(2,1)} fusion(bf16[32064,3072]{1,0:T(8,128)(2,1)} %param.16, s32[1024]{0:T(1024)S(1)} %pad_clamp_fusion), kind=kCustom, calls=%fused_computation | custom fusion | bytes 3146752 | tf_op jit(solution)/shard_map/jit(_take)/gather | solution.py:397
  8.7 61.1 %decoder_layer.1 = bf16[1,64,3072]{2,1,0:T(8,128)(2,1)} custom-call(bf16[256,3072]{1,0:T(8,128)(2,1)} %gather_fusion, s32[1,256]{1,0:T(1,128)} %tok_row.1, s32[1,256]{1,0:T(1,128)} %pos_row.1, f32[256,128]{1,0:T(8,128)} %get-tuple-element.6.cos_tab, f32[256,128]{1,0:T(8,128)} %get-tuple-element.5.sin_tab, bf16[6,3072,128]{2,1,0:T(8,128)(2,1)} %bitcast.12, ...), custom_call_target="tpu_custom_call" | custom-call | tf_op jit(solution)/shard_map/decoder_layer/pallas_call | solution.py:403
  69.8 1.8 %copy.16 = bf16[1,64,3072]{2,1,0:T(8,128)(2,1)} copy(bf16[1,64,3072]{2,1,0:T(8,128)(2,1)} %decoder_layer.1) | data formatting | bytes 786432
  (2 shorter events, 0.0 us)

commit v3 on v2

--- a/solution.py
+++ b/solution.py
@@ -63,18 +63,11 @@
     for i in range(3):
         raw_cps.append(pltpu.make_async_copy(wk_hbm.at[pl.ds(2048 * i, 2048)], wd.at[:, pl.ds(128 * i, 128)], wsem.at[1 + i]))
         raw_cps.append(pltpu.make_async_copy(wv_hbm.at[pl.ds(2048 * i, 2048)], wd.at[:, pl.ds(384 + 128 * i, 128)], wsem.at[4 + i]))
-    for cp in raw_cps:
-        cp.start()
     q_cps = [pltpu.make_async_copy(wq_hbm.at[h], wqkv.at[:, pl.ds(128 * h, 128)], wsem.at[7 + h]) for h in range(6)]
-    for cp in q_cps:
-        cp.start()
     wo_cp = pltpu.make_async_copy(wo_hbm, wo, wsem.at[13])
-    wo_cp.start()
     wg_cp = pltpu.make_async_copy(wg_hbm, wg, wsem.at[14])
     wu_cp = pltpu.make_async_copy(wu_hbm, wu, wsem.at[15])
     wd_cp = pltpu.make_async_copy(wd_hbm, wd, wsem.at[16])
-    wg_cp.start()
-    wu_cp.start()
 
     ids = tok_row[...] - tp * VOCAB_LOCAL
     scale = jnp.where((ids >= 0) & (ids < VOCAB_LOCAL), NORMALIZER, 0.0).astype(F32)
@@ -147,6 +140,8 @@
         for j in range(NRP):
             scale_rows(pl.multiple_of(theirs(k) + ROWP * j, ROWP))
             e_d2d(k, j).start()
+    for cp in raw_cps + q_cps:
+        cp.start()
     for k in range(2):
         for j in range(NRP):
             sl = pl.ds(ROWP * j, ROWP)
@@ -168,7 +163,7 @@
                     wqkv[dst, pl.ds(768 + 256 * w + 128 * h, 128)] = f32buf[pl.ds(h, 256, stride=2), :].astype(BF)
                 return carry
             lax.fori_loop(0, 4, split_heads, 0)
-    wd_cp.start()
+    wo_cp.start()
 
     gain1 = 1.0 + g1[...]
     gain2 = 1.0 + g2[...]
@@ -298,12 +293,15 @@
             out[0, sl, :] = (resid[chip, sl, :].astype(F32) + rms_rows(z, gain4).astype(F32)).astype(BF)
 
     embed_chunk(0)
+    wg_cp.start()
+    wu_cp.start()
     for cp in q_cps:
         cp.wait()
     qkv_chunk(0)
     attend_chunk(0)
     wo_cp.wait()
     out_chunk(0)
+    wd_cp.start()
     embed_chunk(1)
     qkv_chunk(1)
     attend_chunk(1)

time: 71.8 us -> 71.8 us (level)
  no operation moved by 1% of the time
where the time goes in v3:
time: 71.8 us; the launch traced here: 71.5 us
  Pallas kernels  61 us (85%)
  local copies, waits for them, and re-layouts  7.79 us (11%)
  other arithmetic  2.62 us (4%)
    pallas_call x1, Pallas kernels, device_step(): kernel(looked, tokens, positions, cos_tab, sin_tab, w_query.transpose(1,...  61 us
    gather x1, local copies, waits for them, and re-layouts, device_step(): jnp.take(embed_block, jnp.where(in_block, ids, spread), axis=0, mode='clip')  6.03 us
    unnamed x1, local copies, waits for them, and re-layouts  1.77 us

profile of v3, /device:TPU:0, one launch (start us, length us, event | category | flops | bytes accessed | tf_op | source)
XLA Modules:
  0.0 71.5 jit_solution(12860274241164273567)
XLA Ops:
  0.0 0.7 and_select_fusion
  0.7 0.7 convert_element_type.17
  1.4 1.2 %fusion = (f32[256,128]{1,0:T(8,128)}, f32[256,128]{1,0:T(8,128)}) fusion(f32[128]{0:T(128)S(1)} %get-tuple-element.7, f32[128]{0:T(128)S(1)} %get-tuple-element.8, f32[256]{0:T(256)S(1)} %bitcast.20), kind=kLoop, calls=%fused_computation.3 | loop fusion | flops 65536 | bytes 264192 | tf_op jit(solution)/shard_map/mul | solution.py:400
  2.6 6.0 %gather_fusion = bf16[256,3072]{1,0:T(8,128)(2,1)} fusion(bf16[32064,3072]{1,0:T(8,128)(2,1)} %param.16, s32[1024]{0:T(1024)S(1)} %pad_clamp_fusion), kind=kCustom, calls=%fused_computation | custom fusion | bytes 3146752 | tf_op jit(solution)/shard_map/jit(_take)/gather | solution.py:395
  8.7 61.0 %decoder_layer.1 = bf16[1,64,3072]{2,1,0:T(8,128)(2,1)} custom-call(bf16[256,3072]{1,0:T(8,128)(2,1)} %gather_fusion, s32[1,256]{1,0:T(1,128)} %tok_row.1, s32[1,256]{1,0:T(1,128)} %pos_row.1, f32[256,128]{1,0:T(8,128)} %get-tuple-element.6.cos_tab, f32[256,128]{1,0:T(8,128)} %get-tuple-element.5.sin_tab, bf16[6,3072,128]{2,1,0:T(8,128)(2,1)} %bitcast.12, ...), custom_call_target="tpu_custom_call" | custom-call | tf_op jit(solution)/shard_map/decoder_layer/pallas_call | solution.py:401
  69.7 1.8 %copy.16 = bf16[1,64,3072]{2,1,0:T(8,128)(2,1)} copy(bf16[1,64,3072]{2,1,0:T(8,128)(2,1)} %decoder_layer.1) | data formatting | bytes 786432
  (2 shorter events, 0.0 us)

commit v4 on v3

--- a/solution.py
+++ b/solution.py
@@ -95,7 +95,7 @@
         return remote(part.at[pl.ds(theirs(k) + ROWP * j, ROWP)], rd.at[k, pl.ds(ROWP * j, ROWP)], esend.at[k, j], erecv.at[k, j], partner)
 
     def e_x(k, j):
-        sl = pl.ds(ROWP * j, ROWP)
+        sl = pl.ds(QTR * j, QTR)
         return remote(ssum.at[k, sl], rxe.at[k, sl], exsend.at[k, j], exrecv.at[k, j], peer)
 
     def a_d2d(k, j):
@@ -110,9 +110,9 @@
         cs = pl.ds(COLP * n, COLP)
         return remote(part.at[pl.ds(theirs(k), HALF), cs], rd.at[k, :, cs], ysend.at[k, n], yrecv.at[k, n], partner)
 
-    def y_x(k, f, n):
-        sl, cs = pl.ds(QTR * f, QTR), pl.ds(COLP * n, COLP)
-        return remote(ssum.at[k, sl, cs], rxy.at[k, sl, cs], yxsend.at[k, f, n], yxrecv.at[k, f, n], peer)
+    def y_x(k, f):
+        sl = pl.ds(QTR * f, QTR)
+        return remote(ssum.at[k, sl], rxy.at[k, sl], yxsend.at[k, f], yxrecv.at[k, f], peer)
 
     def m_d2d(k, f, j):
         sl = pl.ds(mine(f, k) + ROWP * j, ROWP)
@@ -149,7 +149,8 @@
             scale_rows(row)
             e_d2d(k, j).wait_recv()
             ssum[k, sl, :] = part[pl.ds(row, ROWP), :] + rd[k, sl, :]
-            e_x(k, j).start()
+            if j % 2 == 1:
+                e_x(k, j // 2).start()
 
     for cp in raw_cps:
         cp.wait()
@@ -173,7 +174,8 @@
     def embed_chunk(k):
         for j in range(NRP):
             sl = pl.ds(ROWP * j, ROWP)
-            e_x(k, j).wait_recv()
+            if j % 2 == 0:
+                e_x(k, j // 2).wait_recv()
             emb = ssum[k, sl, :] + rxe[k, sl, :]
             resid[k, sl, :] = emb
             act[pl.ds(pl.multiple_of(own(k) + ROWP * j, ROWP), ROWP), :] = rms_rows(emb.astype(F32), gain1)
@@ -219,14 +221,14 @@
         rows = pl.ds(CHUNK * k, CHUNK)
         for j in range(NRP):
             e_d2d(k, j).wait_send()
-            e_x(k, j).wait_send()
+            if j % 2 == 0:
+                e_x(k, j // 2).wait_send()
             a_d2d(k, j).wait_send()
 
         def finish(n):
             cs = pl.ds(COLP * n, COLP)
             y_d2d(k, n).wait_recv()
             ssum[k, :, cs] = (part[pl.ds(own(k), HALF), cs].astype(F32) + rd[k, :, cs].astype(F32)).astype(BF)
-            y_x(k, 0, n).start()
 
         for n in range(NCP):
             cs = pl.ds(COLP * n, COLP)
@@ -235,12 +237,11 @@
             if n > 0:
                 finish(n - 1)
         finish(NCP - 1)
-        for n in range(NCP):
-            y_x(k, 1, n).start()
+        for f in range(2):
+            y_x(k, f).start()
 
     def mid_block(k, f):
-        for n in range(NCP):
-            y_x(k, f, n).wait_recv()
+        y_x(k, f).wait_recv()
         for j in range(QTR // ROWP):
             sl = pl.ds(QTR * f + ROWP * j, ROWP)
             y = (ssum[k, sl, :].astype(F32) + rxy[k, sl, :].astype(F32)).astype(BF).astype(F32)
@@ -318,8 +319,8 @@
     for k in range(2):
         for n in range(NCP):
             y_d2d(k, n).wait_send()
-            for f in range(2):
-                y_x(k, f, n).wait_send()
+        for f in range(2):
+            y_x(k, f).wait_send()
     down_part(0)
     mid_arrive(1)
     up_part(1, 0, 1)
@@ -374,10 +375,10 @@
             pltpu.VMEM((SEQ, 1), jnp.int32),
             dma((17,)),
             dma((2, NRP)), dma((2, NRP)),
-            dma((2, NRP)), dma((2, NRP)),
+            dma((2, NRP // 2)), dma((2, NRP // 2)),
             dma((2, NRP)), dma((2, NRP)),
             dma((2, NCP)), dma((2, NCP)),
-            dma((2, 2, NCP)), dma((2, 2, NCP)),
+            dma((2, 2)), dma((2, 2)),
             dma((2, 2, QTR // ROWP)), dma((2, 2, QTR // ROWP)),
             dma((2, 2, NCP)), dma((2, 2, NCP)),
             dma((2, NCP)), dma((2, NCP)),

time: 71.8 us -> 73 us (1.017)
  Pallas kernels: 61 us -> 62.2 us
    pallas_call x1, Pallas kernels: 61 us -> 62.2 us  [device_step(): kernel(looked, tokens, positions, cos_tab, sin_tab, w_query.transpose(1,...]
where the time goes in v4:
time: 73 us; the launch traced here: 72.7 us
  Pallas kernels  62.2 us (85%)
  local copies, waits for them, and re-layouts  7.79 us (11%)
  other arithmetic  2.62 us (4%)
    pallas_call x1, Pallas kernels, device_step(): kernel(looked, tokens, positions, cos_tab, sin_tab, w_query.transpose(1,...  62.2 us
    gather x1, local copies, waits for them, and re-layouts, device_step(): jnp.take(embed_block, jnp.where(in_block, ids, spread), axis=0, mode='clip')  6.02 us
    unnamed x1, local copies, waits for them, and re-layouts  1.77 us

profile of v4, /device:TPU:0, one launch (start us, length us, event | category | flops | bytes accessed | tf_op | source)
XLA Modules:
  0.0 72.7 jit_solution(11290543434199572400)
XLA Ops:
  0.0 0.7 and_select_fusion
  0.7 0.7 convert_element_type.17
  1.4 1.2 %fusion = (f32[256,128]{1,0:T(8,128)}, f32[256,128]{1,0:T(8,128)}) fusion(f32[128]{0:T(128)S(1)} %get-tuple-element.7, f32[128]{0:T(128)S(1)} %get-tuple-element.8, f32[256]{0:T(256)S(1)} %bitcast.20), kind=kLoop, calls=%fused_computation.3 | loop fusion | flops 65536 | bytes 264192 | tf_op jit(solution)/shard_map/mul | solution.py:401
  2.6 6.0 %gather_fusion = bf16[256,3072]{1,0:T(8,128)(2,1)} fusion(bf16[32064,3072]{1,0:T(8,128)(2,1)} %param.16, s32[1024]{0:T(1024)S(1)} %pad_clamp_fusion), kind=kCustom, calls=%fused_computation | custom fusion | bytes 3146752 | tf_op jit(solution)/shard_map/jit(_take)/gather | solution.py:396
  8.6 62.2 %decoder_layer.1 = bf16[1,64,3072]{2,1,0:T(8,128)(2,1)} custom-call(bf16[256,3072]{1,0:T(8,128)(2,1)} %gather_fusion, s32[1,256]{1,0:T(1,128)} %tok_row.1, s32[1,256]{1,0:T(1,128)} %pos_row.1, f32[256,128]{1,0:T(8,128)} %get-tuple-element.6.cos_tab, f32[256,128]{1,0:T(8,128)} %get-tuple-element.5.sin_tab, bf16[6,3072,128]{2,1,0:T(8,128)(2,1)} %bitcast.12, ...), custom_call_target="tpu_custom_call" | custom-call | tf_op jit(solution)/shard_map/decoder_layer/pallas_call | solution.py:402
  70.9 1.8 %copy.16 = bf16[1,64,3072]{2,1,0:T(8,128)(2,1)} copy(bf16[1,64,3072]{2,1,0:T(8,128)(2,1)} %decoder_layer.1) | data formatting | bytes 786432
  (2 shorter events, 0.0 us)
